TPU v7x, 32 devices: a whole 2x2x4 slice. The times are simulated.
32 devices in a mesh: freq: 4 (over y, x), rows: 8 (over z, core).
Axes of the slice: x: 2, y: 2, z: 4, core: 2. Of those that a mesh axis runs over, the one named last changes fastest.
Arguments:
- coupling: bfloat16 [8192, 8192], P('rows'), may hold values from -1 to 1
- delays: int32 [8192, 8192], P('rows'), may hold values from 0 to 63
- freq_index: int32 [4], P('freq'), parts along dimension 0, may hold values from 0 to 255
- initial: float32 [4, 2, 8192], P('freq', None, 'rows'), parts along dimension 0, may hold values from -6 to 6
Outputs:
- eigvector: float32 [4, 2, 8192], P('freq', None, 'rows'), parts along dimension 0
- eigvalue: float32 [4, 2], P('freq'), parts along dimension 0
There are 4 independent parts, one for each index of `freq`. A program takes and returns all parts, laid end to end along the dimension named above; an argument that names none is the same for every part. Nothing has to cross between parts.
All inputs are finite; a program needn't handle non-finite values.
Results may differ from a plain program's by a relative error of at most 0.0003.
Values sent between devices are 32-bit elements; how exact they have to be, the bound alone decides.
No kernel may reach another device: no remote copies, remote signals or barrier semaphores. Data moves between devices by JAX's collectives and lax.ppermute only.
A program may use at most 192 MiB of HBM per device.

v0:
```python
import math

import jax
import jax.numpy as jnp
from jax import lax
from jax.sharding import PartitionSpec as P

N = 8192
FTOTAL = 256
ITERS = 4


EPS = 1e-06


def build_operator(coupling, delays, which_freq):
    step_count = which_freq + 1
    residue = jnp.remainder(step_count * delays, 2 * FTOTAL)
    phase_angle = residue.astype(jnp.float32) * (math.pi / FTOTAL)
    weights = coupling.astype(jnp.float32)
    real_part = -weights * jnp.cos(phase_angle)
    imag_part = weights * jnp.sin(phase_angle)
    angular = step_count.astype(jnp.float32) * (math.pi / FTOTAL)
    return (real_part, imag_part, angular)


def product(real_part, imag_part, angular, gathered, own_rows):
    real_prod = jnp.dot(
        real_part, gathered.T, precision=lax.Precision.HIGHEST, preferred_element_type=jnp.float32
    )
    imag_prod = jnp.dot(
        imag_part, gathered.T, precision=lax.Precision.HIGHEST, preferred_element_type=jnp.float32
    )
    new_real = real_prod[:, 0] - imag_prod[:, 1] - angular * own_rows[1]
    new_imag = real_prod[:, 1] + imag_prod[:, 0] + angular * own_rows[0]
    return jnp.stack([new_real, new_imag], axis=0)


def power(coupling, delays, indices, first):
    real_all, imag_all, angular_all = lax.map(
        lambda which: build_operator(coupling, delays, which), indices
    )
    iterate = first
    previous_whole = first
    whole_iterate = first
    divisor = jnp.ones((first.shape[0], 1, 1), jnp.float32)
    for sweep in range(ITERS + 1):
        whole_iterate = lax.all_gather(iterate, "rows", axis=2, tiled=True)
        squares = jnp.sum(whole_iterate * whole_iterate, axis=(1, 2))
        divisor = jnp.sqrt(squares / N + EPS)[:, None, None]
        if sweep < ITERS:
            normed = iterate / divisor
            previous_whole = whole_iterate / divisor
            iterate = lax.map(
                lambda packed: product(packed[0], packed[1], packed[2], packed[3], packed[4]),
                (real_all, imag_all, angular_all, previous_whole, normed),
            )
    dot_real = jnp.sum(
        previous_whole[:, 0] * whole_iterate[:, 0] + previous_whole[:, 1] * whole_iterate[:, 1],
        axis=1,
    )
    dot_imag = jnp.sum(
        previous_whole[:, 0] * whole_iterate[:, 1] - previous_whole[:, 1] * whole_iterate[:, 0],
        axis=1,
    )
    result = iterate / divisor
    estimate = jnp.stack([dot_real, dot_imag], axis=1) / N
    return (result, estimate)


def shards(coupling, delays, freq_index, initial):

    def visit(carry, packed):
        which_freq, first = packed
        result, estimate = power(coupling, delays, which_freq[None], first[None])
        return (carry, (result[0], estimate[0]))

    unused, outputs = lax.scan(visit, jnp.int32(0), (freq_index, initial))
    eigvector, eigvalue = outputs
    return (eigvector, eigvalue)


def solution(mesh):
    return jax.shard_map(
        shards,
        mesh=mesh,
        in_specs=(P("rows", None), P("rows", None), P("freq"), P("freq", None, "rows")),
        out_specs=(P("freq", None, "rows"), P("freq", None)),
        check_vma=False,
    )
```

profile of v0, /device:TPU:0, one launch (start us, length us, event | category | flops | bytes accessed | tf_op | source)
XLA Modules:
  0.0 479.1 jit_solution(772224042721452039)
XLA Ops:
  1.3 15.9 %all_gather.20 = f32[1,2,8192]{2,1,0:T(2,128)S(1)} all-gather(f32[1,2,1024]{2,1,0:T(2,128)} %param.7), channel_id=1, replica_groups=mesh['freq'=4,'rows'=8] {'rows'}, dimensions={2}, use_global_device_ids=true | all-gather | bytes 73728 | tf_op jit(solution)/shard_map/while/body/eval_jaxpr/all_gather | solution.py:48
  17.2 0.7 multiply_reduce_fusion.4
  18.5 0.7 broadcast_divide_fusion.4
  19.3 138.6 %fusion = (f32[1024,8192]{1,0:T(8,128)}, f32[1024,8192]{1,0:T(8,128)}) fusion(bf16[1024,8192]{1,0:T(8,128)(2,1)} %param.4, s32[1024,8192]{1,0:T(8,128)} %param.5, s32[]{:T(128)} %bitcast), kind=kLoop, calls=%fused_computation.5 | loop fusion | flops 150994944 | bytes 117440512 | tf_op jit(solution)/shard_map/while/body/eval_jaxpr/while/body/eval_jaxpr/mul | solution.py:21
  157.8 31.9 %fusion.6 = f32[1024,2]{0,1:T(2,128)S(1)} fusion(f32[1024,8192]{1,0:T(8,128)} %get-tuple-element.181, f32[1,2,8192]{2,1,0:T(2,128)S(1)} %all_gather.20, f32[]{:T(128)S(6)} %sqrt.25), kind=kOutput, calls=%fused_computation.11 | convolution fusion | flops 201342976 | bytes 33628164 | tf_op jit(solution)/shard_map/while/body/eval_jaxpr/while/body/eval_jaxpr/dot_general | solution.py:28
  189.7 32.3 %fusion.4 = f32[1024,2]{0,1:T(2,128)S(1)} fusion(f32[1024,8192]{1,0:T(8,128)} %get-tuple-element.182, f32[1,2,8192]{2,1,0:T(2,128)S(1)} %all_gather.20, f32[]{:T(128)S(6)} %sqrt.25), kind=kOutput, calls=%fused_computation.9 | convolution fusion | flops 201342976 | bytes 33628164 | tf_op jit(solution)/shard_map/while/body/eval_jaxpr/while/body/eval_jaxpr/dot_general | solution.py:31
  222.1 14.0 %all-gather = f32[2,8192]{1,0:T(2,128)S(1)} all-gather(f32[2,1024]{1,0:T(2,128)S(1)} %pad_maximum_fusion), channel_id=2, replica_groups=mesh['freq'=4,'rows'=8] {'rows'}, dimensions={1}, use_global_device_ids=true | all-gather | bytes 73728 | tf_op jit(solution)/shard_map/while/body/eval_jaxpr/all_gather | solution.py:48
  236.1 0.7 multiply_reduce_fusion.2
  237.4 32.0 %fusion.8 = f32[1024,2]{0,1:T(2,128)S(1)} fusion(f32[1024,8192]{1,0:T(8,128)} %get-tuple-element.181, f32[2,8192]{1,0:T(2,128)S(1)} %all-gather, f32[]{:T(128)S(6)} %sqrt.26), kind=kOutput, calls=%fused_computation.66 | convolution fusion | flops 201342976 | bytes 33628164 | tf_op jit(solution)/shard_map/while/body/eval_jaxpr/while/body/eval_jaxpr/dot_general | solution.py:28
  269.5 31.9 %fusion.9 = f32[1024,2]{0,1:T(2,128)S(1)} fusion(f32[1024,8192]{1,0:T(8,128)} %get-tuple-element.182, f32[2,8192]{1,0:T(2,128)S(1)} %all-gather, f32[]{:T(128)S(6)} %sqrt.26), kind=kOutput, calls=%fused_computation.67 | convolution fusion | flops 201342976 | bytes 33628164 | tf_op jit(solution)/shard_map/while/body/eval_jaxpr/while/body/eval_jaxpr/dot_general | solution.py:31
  301.4 14.0 %all-gather.1 = f32[2,8192]{1,0:T(2,128)S(1)} all-gather(f32[2,1024]{1,0:T(2,128)S(1)} %pad_maximum_fusion.1), channel_id=3, replica_groups=mesh['freq'=4,'rows'=8] {'rows'}, dimensions={1}, use_global_device_ids=true | all-gather | bytes 73728 | tf_op jit(solution)/shard_map/while/body/eval_jaxpr/all_gather | solution.py:48
  315.4 0.7 multiply_reduce_fusion.1
  316.8 32.3 %fusion.10 = f32[1024,2]{0,1:T(2,128)S(1)} fusion(f32[1024,8192]{1,0:T(8,128)} %get-tuple-element.181, f32[2,8192]{1,0:T(2,128)S(1)} %all-gather.1, f32[]{:T(128)S(6)} %sqrt.27), kind=kOutput, calls=%fused_computation.68 | convolution fusion | flops 201342976 | bytes 33628164 | tf_op jit(solution)/shard_map/while/body/eval_jaxpr/while/body/eval_jaxpr/dot_general | solution.py:28
  349.0 31.9 %fusion.11 = f32[1024,2]{0,1:T(2,128)S(1)} fusion(f32[1024,8192]{1,0:T(8,128)} %get-tuple-element.182, f32[2,8192]{1,0:T(2,128)S(1)} %all-gather.1, f32[]{:T(128)S(6)} %sqrt.27), kind=kOutput, calls=%fused_computation.69 | convolution fusion | flops 201342976 | bytes 33628164 | tf_op jit(solution)/shard_map/while/body/eval_jaxpr/while/body/eval_jaxpr/dot_general | solution.py:31
  381.0 14.0 %all-gather.2 = f32[2,8192]{1,0:T(2,128)S(1)} all-gather(f32[2,1024]{1,0:T(2,128)S(1)} %pad_maximum_fusion.2), channel_id=4, replica_groups=mesh['freq'=4,'rows'=8] {'rows'}, dimensions={1}, use_global_device_ids=true | all-gather | bytes 73728 | tf_op jit(solution)/shard_map/while/body/eval_jaxpr/all_gather | solution.py:48
  395.0 0.7 multiply_reduce_fusion
  396.3 32.0 %fusion.13 = f32[1024,2]{0,1:T(2,128)S(1)} fusion(f32[1024,8192]{1,0:T(8,128)} %get-tuple-element.182, f32[2,8192]{1,0:T(2,128)S(1)} %all-gather.2, f32[]{:T(128)S(6)} %sqrt.28), kind=kOutput, calls=%fused_computation.71 | convolution fusion | flops 201342976 | bytes 33628164 | tf_op jit(solution)/shard_map/while/body/eval_jaxpr/while/body/eval_jaxpr/dot_general | solution.py:31
  428.4 31.9 %fusion.12 = f32[1024,2]{0,1:T(2,128)S(1)} fusion(f32[1024,8192]{1,0:T(8,128)} %get-tuple-element.181, f32[2,8192]{1,0:T(2,128)S(1)} %all-gather.2, f32[]{:T(128)S(6)} %sqrt.28), kind=kOutput, calls=%fused_computation.70 | convolution fusion | flops 201342976 | bytes 33628164 | tf_op jit(solution)/shard_map/while/body/eval_jaxpr/while/body/eval_jaxpr/dot_general | solution.py:28
  460.4 14.0 %all-gather.3 = f32[2,8192]{1,0:T(2,128)S(1)} all-gather(f32[2,1024]{1,0:T(2,128)S(1)} %pad_maximum_fusion.3), channel_id=5, replica_groups=mesh['freq'=4,'rows'=8] {'rows'}, dimensions={1}, use_global_device_ids=true | all-gather | bytes 73728 | tf_op jit(solution)/shard_map/while/body/eval_jaxpr/all_gather | solution.py:48
  474.4 0.7 multiply_reduce_fusion.3
  475.7 0.6 maximum_divide_fusion.3
  476.3 0.8 add_reduce_fusion
  477.1 1.8 maximum_multiply_fusion
  (16 shorter events, 0.3 us)
where the time goes:
time: 486 us; the launch traced here: 479 us
  matrix products  256 us (53%)
  other arithmetic  146 us (30%)
  blocking collectives  71.9 us (15%)
  between operations  5.07 us (1%)
    mul x1, other arithmetic, build_operator(): real_part = -weights * jnp.cos(phase_angle)  139 us
    dot_general x4, matrix products, product(): jnp.dot(imag_part, gathered.T, precision=lax.Precision.HIGHEST, preferred...  128 us
    dot_general x4, matrix products, product(): jnp.dot(real_part, gathered.T, precision=lax.Precision.HIGHEST, preferred...  128 us
    all_gather x5, blocking collectives, power(): whole_iterate = lax.all_gather(iterate, 'rows', axis=2, tiled=True)  71.9 us

commit v1 on v0

v1 whole, which is shorter than its diff:
```python
import functools
import math

import jax
import jax.numpy as jnp
from jax import lax
from jax.experimental import pallas as pl
from jax.experimental.pallas import tpu as pltpu
from jax.sharding import PartitionSpec as P

FTOTAL = 256
ITERS = 4
EPS = 1e-06

F32 = jnp.float32
HIGH = jnp.bfloat16
LOW = jnp.float8_e4m3fn
SCALE = 2.0**17
VMEM = pl.BlockSpec(memory_space=pltpu.VMEM)
SMEM = pl.BlockSpec(memory_space=pltpu.SMEM)
ANY = pl.BlockSpec(memory_space=pl.ANY)
SUB, LANE, FINE = 8, 128, 8
GRANT = 8 * 2**20
CHUNK = 2048


def gather_rows(table, index):
    dims = lax.GatherDimensionNumbers(
        offset_dims=(),
        collapsed_slice_dims=(0,),
        start_index_map=(0,),
        operand_batching_dims=(1,),
        start_indices_batching_dims=(1,),
    )
    return lax.gather(
        table,
        index[..., None],
        dims,
        slice_sizes=(1, 1),
        mode=lax.GatherScatterMode.PROMISE_IN_BOUNDS,
    )


def tables(step_count):
    entry = lax.broadcasted_iota(jnp.int32, (SUB, LANE), 0)

    def angle(times):
        residue = (step_count * (entry * times)) & (2 * FTOTAL - 1)
        return residue.astype(F32) * (math.pi / FTOTAL)

    fine, coarse = angle(1), angle(FINE)
    fine_cos = jnp.cos(fine)
    fine_cos = jnp.where(jnp.abs(fine_cos) < 1e-6, 1e-6, fine_cos)
    return jnp.cos(coarse), jnp.sin(coarse), fine_cos * SCALE, jnp.sin(fine) / fine_cos


def build_operator(rows, strip, step_count, c_hbm, d_hbm, hi_ref, lo_ref, c_buf, d_buf, c_sem, d_sem):
    total, width = c_hbm.shape
    blocks = total // rows

    def copies(block, slot):
        here = pl.ds(pl.multiple_of(block * rows, rows), rows)
        return (
            pltpu.make_async_copy(c_hbm.at[here], c_buf.at[slot], c_sem.at[slot]),
            pltpu.make_async_copy(d_hbm.at[here], d_buf.at[slot], d_sem.at[slot]),
        )

    for copy in copies(0, 0):
        copy.start()
    coarse_cos, coarse_sin, fine_cos, fine_tan = tables(step_count)

    def block_body(block, carry):
        slot = lax.rem(block, 2)
        for copy in copies(block, slot):
            copy.wait()

        @pl.when(block + 1 < blocks)
        def _():
            for copy in copies(block + 1, 1 - slot):
                copy.start()

        def strip_body(at, carry):
            for row in range(0, rows, 32):
                for lane in range(0, strip, LANE):
                    here = pl.ds(pl.multiple_of(at * strip + lane, LANE), LANE)
                    weight = c_buf[slot, row : row + 32, here].astype(F32)
                    delay = d_buf[slot, row : row + 32, here]
                    reals, imags = [], []
                    for sub in range(0, 32, SUB):
                        bins = delay[sub : sub + SUB]
                        low, high = bins & (FINE - 1), bins >> 3
                        cos_l, tan_l = gather_rows(fine_cos, low), gather_rows(fine_tan, low)
                        cos_h, sin_h = gather_rows(coarse_cos, high), gather_rows(coarse_sin, high)
                        size = weight[sub : sub + SUB] * cos_l
                        reals.append(size * (cos_h - sin_h * tan_l))
                        imags.append(size * (sin_h + cos_h * tan_l))
                    to = pl.ds(pl.multiple_of(block * rows + row, 32), 32)
                    for plane, parts in ((0, reals), (1, imags)):
                        value = jnp.concatenate(parts, axis=0)
                        hi = value.astype(HIGH)
                        hi_ref[plane, to, here] = hi
                        lo_ref[plane, to, here] = (value - hi.astype(F32)).astype(LOW)
            return carry

        lax.fori_loop(0, width // strip, strip_body, 0)
        return carry

    lax.fori_loop(0, blocks, block_body, 0)


def split(value):
    first = value.astype(HIGH).astype(F32)
    second = (value - first).astype(HIGH).astype(F32)
    third = (value - first - second).astype(HIGH).astype(F32)
    return first, second, third


def advance(chunk, step_count, z_ref, hi_ref, lo_ref, left_c, left_s):
    peers, _, own = z_ref.shape
    nodes = peers * own
    whole = z_ref[0] * z_ref[0]
    for peer in range(1, peers):
        whole = whole + z_ref[peer] * z_ref[peer]
    squares = jnp.sum(jnp.sum(whole, axis=1, keepdims=True), axis=0, keepdims=True)
    inverse = 1.0 / jnp.sqrt(squares / nodes + EPS)
    for peer in range(peers):
        here = slice(peer * own, (peer + 1) * own)
        normed = z_ref[peer] * inverse
        turned = jnp.concatenate([-normed[1:2], normed[0:1]], axis=0)
        for left, value in ((left_c, -normed), (left_s, turned)):
            pad = jnp.zeros((16 - 6, own), F32)
            left[:, here] = jnp.concatenate([*split(value), pad], axis=0).astype(HIGH)

    def step(at, totals):
        here = pl.ds(pl.multiple_of(at * chunk, chunk), chunk)
        for plane, left in ((0, left_c), (1, left_s)):
            for matrix in (hi_ref, lo_ref):
                totals = totals + lax.dot_general(
                    left[:, here],
                    matrix[plane, :, here],
                    (((1,), (1,)), ((), ())),
                    preferred_element_type=F32,
                )
        return totals

    totals = lax.fori_loop(0, nodes // chunk, step, jnp.zeros((16, own), F32))
    product = (totals[0:2] + totals[2:4] + totals[4:6]) * (1.0 / SCALE)
    mine = z_ref[lax.axis_index("rows")] * inverse
    turned = jnp.concatenate([-mine[1:2], mine[0:1]], axis=0)
    angular = step_count.astype(F32) * (math.pi / FTOTAL)
    return mine, turned, product + angular * turned


def first_kernel(rows, strip, chunk, q_ref, z_hbm, c_hbm, d_hbm, out_ref, hi_ref, lo_ref, z_buf, left_c, left_s, z_sem, *scratch):
    fetch = pltpu.make_async_copy(z_hbm, z_buf, z_sem)
    fetch.start()
    step_count = q_ref[0] + 1
    build_operator(rows, strip, step_count, c_hbm, d_hbm, hi_ref, lo_ref, *scratch)
    fetch.wait()
    _, _, new = advance(chunk, step_count, z_buf, hi_ref, lo_ref, left_c, left_s)
    for peer in range(out_ref.shape[0]):
        out_ref[peer] = new


def next_kernel(chunk, q_ref, z_ref, hi_ref, lo_ref, out_ref, left_c, left_s):
    _, _, new = advance(chunk, q_ref[0] + 1, z_ref, hi_ref, lo_ref, left_c, left_s)
    for peer in range(out_ref.shape[0]):
        out_ref[peer] = new


def last_kernel(chunk, q_ref, z_ref, hi_ref, lo_ref, out_ref, sums_ref, left_c, left_s):
    mine, turned, new = advance(chunk, q_ref[0] + 1, z_ref, hi_ref, lo_ref, left_c, left_s)
    out_ref[...] = new

    def summed(value):
        return jnp.sum(jnp.sum(value, axis=1, keepdims=True), axis=0, keepdims=True)

    row = lax.broadcasted_iota(jnp.int32, (SUB, LANE), 0)
    sums = jnp.where(row == 0, summed(new * new), 0.0)
    sums = sums + jnp.where(row == 1, summed(mine * new), 0.0)
    sums = sums + jnp.where(row == 2, summed(turned * new), 0.0)
    for peer in range(sums_ref.shape[0]):
        sums_ref[peer] = sums


def first(step, z, coupling, delays):
    rows, strip = 64, 256
    total, width = coupling.shape
    shape = (2, total, width)
    return pl.pallas_call(
        functools.partial(first_kernel, rows, strip, min(CHUNK, width)),
        out_shape=(
            jax.ShapeDtypeStruct(z.shape, F32),
            pltpu.VMEM(shape, HIGH),
            pltpu.VMEM(shape, LOW),
        ),
        in_specs=[SMEM, ANY, ANY, ANY],
        out_specs=(VMEM, VMEM, VMEM),
        scratch_shapes=[
            pltpu.VMEM(z.shape, F32),
            pltpu.VMEM((16, width), HIGH),
            pltpu.VMEM((16, width), HIGH),
            pltpu.SemaphoreType.DMA,
            pltpu.VMEM((2, rows, width), coupling.dtype),
            pltpu.VMEM((2, rows, width), delays.dtype),
            pltpu.SemaphoreType.DMA((2,)),
            pltpu.SemaphoreType.DMA((2,)),
        ],
        compiler_params=pltpu.CompilerParams(vmem_limit_bytes=GRANT),
        name="first",
    )(step, z, coupling, delays)


def apply(kernel, outputs, step, z, hi, lo):
    nodes = z.shape[0] * z.shape[2]
    return pl.pallas_call(
        functools.partial(kernel, min(CHUNK, nodes)),
        out_shape=tuple(jax.ShapeDtypeStruct(shape, F32) for shape in outputs),
        in_specs=[SMEM, VMEM, VMEM, VMEM],
        out_specs=(VMEM,) * len(outputs),
        scratch_shapes=[pltpu.VMEM((16, nodes), HIGH), pltpu.VMEM((16, nodes), HIGH)],
        compiler_params=pltpu.CompilerParams(vmem_limit_bytes=GRANT),
        name="apply",
    )(step, z, hi, lo)


def finish_kernel(nodes, y_ref, sums_ref, vector_ref, value_ref):
    sums = jnp.sum(sums_ref[...], axis=0)
    vector_ref[...] = y_ref[...] * (1.0 / jnp.sqrt(sums[0:1, 0:1] / nodes + EPS))
    lane = lax.broadcasted_iota(jnp.int32, (1, LANE), 1)
    value_ref[...] = jnp.where(lane == 0, sums[1:2], sums[2:3]) * (1.0 / nodes)


def finish(nodes, y, sums):
    return pl.pallas_call(
        functools.partial(finish_kernel, nodes),
        out_shape=(jax.ShapeDtypeStruct(y.shape, F32), jax.ShapeDtypeStruct((1, LANE), F32)),
        in_specs=[VMEM, VMEM],
        out_specs=(VMEM, VMEM),
        name="finish",
    )(y, sums)


def exchange(value):
    return lax.all_to_all(value, "rows", 0, 0, tiled=True)


def solution(mesh):
    peers = mesh.shape["rows"]

    def point(coupling, delays, step, start):
        nodes = coupling.shape[1]
        z = exchange(jnp.broadcast_to(start[None], (peers, *start.shape)))
        y, hi, lo = first(step, z, coupling, delays)
        hi = pltpu.with_memory_space_constraint(hi, pltpu.VMEM)
        lo = pltpu.with_memory_space_constraint(lo, pltpu.VMEM)
        for sweep in range(1, ITERS - 1):
            (y,) = apply(next_kernel, [z.shape], step, exchange(y), hi, lo)
        y, sums = apply(last_kernel, [z.shape[1:], (peers, SUB, LANE)], step, exchange(y), hi, lo)
        return finish(nodes, y, exchange(sums))

    def shards(coupling, delays, freq_index, initial):
        vectors, values = [], []
        for at in range(freq_index.shape[0]):
            vector, value = point(coupling, delays, freq_index[at : at + 1], initial[at])
            vectors.append(vector)
            values.append(value[0, 0:2])
        return jnp.stack(vectors), jnp.stack(values)

    return jax.shard_map(
        shards,
        mesh=mesh,
        in_specs=(P("rows", None), P("rows", None), P("freq"), P("freq", None, "rows")),
        out_specs=(P("freq", None, "rows"), P("freq", None)),
        check_vma=False,
    )
```

time: 486 us -> 151 us (0.31); the launches traced: 479 us -> 150 us
  matrix products: 256 us -> 0 us
  other arithmetic: 146 us -> 0 us
  Pallas kernels: 0 us -> 96 us
  blocking collectives: 71.9 us -> 39.3 us
  starting transfers between devices: 0 us -> 6.35 us
  waiting for transfers between devices: 0 us -> 5.27 us
    dot_general x8 -> x0, matrix products: 256 us -> none  [the longest x4 128 us: product(): jnp.dot(imag_part, gathered.T, precision=lax.Precision.HIGHEST, preferred...]
    mul x1 -> x0, other arithmetic: 139 us -> none  [build_operator(): real_part = -weights * jnp.cos(phase_angle)]
    pallas_call x0 -> x5, Pallas kernels: none -> 96 us  [the longest x1 48.7 us: first(): pl.pallas_call(functools.partial(first_kernel, rows, strip, min(CHUNK, wi...]
    all_gather x5 -> x0, blocking collectives: 71.9 us -> none  [power(): whole_iterate = lax.all_gather(iterate, 'rows', axis=2, tiled=True)]
    all_to_all x0 -> x4, blocking collectives: none -> 39.3 us  [exchange(): return lax.all_to_all(value, 'rows', 0, 0, tiled=True)]
    all_to_all x0 -> x1, starting transfers between devices: none -> 6.35 us  [exchange(): return lax.all_to_all(value, 'rows', 0, 0, tiled=True)]
    all_to_all x0 -> x1, waiting for transfers between devices: none -> 5.27 us  [exchange(): return lax.all_to_all(value, 'rows', 0, 0, tiled=True)]
  transfers between devices with their start and end apart: 0 -> 1, of which waited for: 0 -> 1; matrix products, arithmetic and copies ran while one was open for 0% -> 0% of each run, Pallas kernels for 0% -> 0%
where the time goes in v1:
time: 151 us; the launch traced here: 150 us
  Pallas kernels  96 us (64%)
  blocking collectives  39.3 us (26%)
  starting transfers between devices  6.35 us (4%)
  waiting for transfers between devices  5.27 us (3%)
  local copies, waits for them, and re-layouts  1.95 us (1%)
    pallas_call x1, Pallas kernels, first(): pl.pallas_call(functools.partial(first_kernel, rows, strip, min(CHUNK, wi...  48.7 us
    pallas_call x3, Pallas kernels, apply(): pl.pallas_call(functools.partial(kernel, min(CHUNK, nodes)), out_shape=tu...  45.9 us
    all_to_all x4, blocking collectives, exchange(): return lax.all_to_all(value, 'rows', 0, 0, tiled=True)  39.3 us
    all_to_all x1, starting transfers between devices, exchange(): return lax.all_to_all(value, 'rows', 0, 0, tiled=True)  6.35 us
    all_to_all x1, waiting for transfers between devices, exchange(): return lax.all_to_all(value, 'rows', 0, 0, tiled=True)  5.27 us
  transfers between devices with their start and end apart: 1, of which 1 were waited for; matrix products, arithmetic and copies ran while one was open for 0% of the time, Pallas kernels for 0%

profile of v1, /device:TPU:0, one launch (start us, length us, event | category | flops | bytes accessed | tf_op | source)
XLA Modules:
  0.0 150.2 jit_solution(12201005536327866903)
XLA Ops:
  0.6 1.3 broadcast_in_dim.8
  2.0 6.4 %all-to-all-start = ((f32[8,2,1024]{2,1,0:T(2,128)}), f32[8,2,1024]{2,1,0:T(2,128)S(1)}, u32[]{:S(2)}, u32[]{:S(2)}) async-start(f32[8,2,1024]{2,1,0:T(2,128)} %broadcast_in_dim.8), calls=%async_computation | async-start | bytes 131072 | tf_op jit(solution)/shard_map/all_to_all | solution.py:245
  9.0 5.3 %all-to-all-done.z_hbm = f32[8,2,1024]{2,1,0:T(2,128)S(1)} async-done(((f32[8,2,1024]{2,1,0:T(2,128)}), f32[8,2,1024]{2,1,0:T(2,128)S(1)}, u32[]{:S(2)}, u32[]{:S(2)}) %all-to-all-start) | async-done | bytes 65568 | tf_op jit(solution)/shard_map/all_to_all | solution.py:245
  14.2 0.0 copy-start
  14.2 0.6 copy-done
  14.9 48.7 %first.1 = (f32[8,2,1024]{2,1,0:T(2,128)}, bf16[2,1024,8192]{2,1,0:T(8,128)(2,1)S(1)}, f8e4m3fn[2,1024,8192]{2,1,0:T(32,128)(4,1)S(1)}) custom-call(s32[1]{0:T(128)S(6)} %copy.6.q_ref, f32[8,2,1024]{2,1,0:T(2,128)} %copy-done, bf16[1024,8192]{1,0:T(8,128)(2,1)} %c_hbm.1, s32[1024,8192]{1,0:T(8,128)} %d_hbm.1), custom_call_target="tpu_custom_call" | custom-call | tf_op jit(solution)/shard_map/first/pallas_call | solution.py:190
  63.6 9.9 %all_to_all.25.z_ref = f32[8,2,1024]{2,1,0:T(2,128)} all-to-all(f32[8,2,1024]{2,1,0:T(2,128)} %get-tuple-element.9), channel_id=1, replica_groups=mesh['freq'=4,'rows'=8] {'rows'}, dimensions={0} | all-to-all | bytes 131072 | tf_op jit(solution)/shard_map/all_to_all | solution.py:245
  73.4 15.3 %apply.3 = f32[8,2,1024]{2,1,0:T(2,128)} custom-call(s32[1]{0:T(128)S(6)} %copy.6.q_ref, f32[8,2,1024]{2,1,0:T(2,128)} %all_to_all.25.z_ref, bf16[2,1024,8192]{2,1,0:T(8,128)(2,1)S(1)} %get-tuple-element.10.hi_ref, f8e4m3fn[2,1024,8192]{2,1,0:T(32,128)(4,1)S(1)} %get-tuple-element.11.lo_ref), custom_call_target="tpu_custom_call" | custom-call | tf_op jit(solution)/shard_map/apply/pallas_call | solution.py:216
  88.7 9.9 %all_to_all.26.z_ref = f32[8,2,1024]{2,1,0:T(2,128)} all-to-all(f32[8,2,1024]{2,1,0:T(2,128)} %apply.3), channel_id=1, replica_groups=mesh['freq'=4,'rows'=8] {'rows'}, dimensions={0} | all-to-all | bytes 131072 | tf_op jit(solution)/shard_map/all_to_all | solution.py:245
  98.6 15.3 %apply.4 = f32[8,2,1024]{2,1,0:T(2,128)} custom-call(s32[1]{0:T(128)S(6)} %copy.6.q_ref, f32[8,2,1024]{2,1,0:T(2,128)} %all_to_all.26.z_ref, bf16[2,1024,8192]{2,1,0:T(8,128)(2,1)S(1)} %get-tuple-element.10.hi_ref, f8e4m3fn[2,1024,8192]{2,1,0:T(32,128)(4,1)S(1)} %get-tuple-element.11.lo_ref), custom_call_target="tpu_custom_call" | custom-call | tf_op jit(solution)/shard_map/apply/pallas_call | solution.py:216
  113.9 9.9 %all_to_all.27.z_ref = f32[8,2,1024]{2,1,0:T(2,128)} all-to-all(f32[8,2,1024]{2,1,0:T(2,128)} %apply.4), channel_id=1, replica_groups=mesh['freq'=4,'rows'=8] {'rows'}, dimensions={0} | all-to-all | bytes 131072 | tf_op jit(solution)/shard_map/all_to_all | solution.py:245
  123.7 15.4 %apply.5 = (f32[2,1024]{1,0:T(2,128)}, f32[8,8,128]{2,1,0:T(8,128)}) custom-call(s32[1]{0:T(128)S(6)} %copy.6.q_ref, f32[8,2,1024]{2,1,0:T(2,128)} %all_to_all.27.z_ref, bf16[2,1024,8192]{2,1,0:T(8,128)(2,1)S(1)} %get-tuple-element.10.hi_ref, f8e4m3fn[2,1024,8192]{2,1,0:T(32,128)(4,1)S(1)} %get-tuple-element.11.lo_ref), custom_call_target="tpu_custom_call" | custom-call | tf_op jit(solution)/shard_map/apply/pallas_call | solution.py:216
  139.1 9.7 %all_to_all.28.sums_ref = f32[8,8,128]{2,1,0:T(8,128)} all-to-all(f32[8,8,128]{2,1,0:T(8,128)} %get-tuple-element.13), channel_id=1, replica_groups=mesh['freq'=4,'rows'=8] {'rows'}, dimensions={0} | all-to-all | bytes 65536 | tf_op jit(solution)/shard_map/all_to_all | solution.py:245
  148.8 1.4 finish.1
Async XLA Ops:
  2.0 12.3 %all-to-all-start = ((f32[8,2,1024]{2,1,0:T(2,128)}), f32[8,2,1024]{2,1,0:T(2,128)S(1)}, u32[]{:S(2)}, u32[]{:S(2)}) async-start(f32[8,2,1024]{2,1,0:T(2,128)} %broadcast_in_dim.8), calls=%async_computation | async-start | bytes 131072 | tf_op jit(solution)/shard_map/all_to_all | solution.py:245
  14.2 0.6 copy-start

commit v2 on v1

v2 whole, which is shorter than its diff:
```python
import functools
import math

import jax
import jax.numpy as jnp
from jax import lax
from jax.experimental import pallas as pl
from jax.experimental.pallas import tpu as pltpu
from jax.sharding import PartitionSpec as P

FTOTAL = 256
ITERS = 4
EPS = 1e-06

F32 = jnp.float32
HIGH = jnp.bfloat16
LOW = jnp.float8_e4m3fn
SCALE = 2.0**17
VMEM = pl.BlockSpec(memory_space=pltpu.VMEM)
SMEM = pl.BlockSpec(memory_space=pltpu.SMEM)
ANY = pl.BlockSpec(memory_space=pl.ANY)
SUB, LANE, FINE = 8, 128, 8
GRANT = 8 * 2**20
CHUNK = 2048
SLAB = 512


def gather_rows(table, index):
    dims = lax.GatherDimensionNumbers(
        offset_dims=(),
        collapsed_slice_dims=(0,),
        start_index_map=(0,),
        operand_batching_dims=(1,),
        start_indices_batching_dims=(1,),
    )
    return lax.gather(
        table,
        index[..., None],
        dims,
        slice_sizes=(1, 1),
        mode=lax.GatherScatterMode.PROMISE_IN_BOUNDS,
    )


def tables(step_count):
    entry = lax.broadcasted_iota(jnp.int32, (SUB, LANE), 0)

    def angle(times):
        residue = (step_count * (entry * times)) & (2 * FTOTAL - 1)
        return residue.astype(F32) * (math.pi / FTOTAL)

    fine, coarse = angle(1), angle(FINE)
    fine_cos = jnp.cos(fine)
    fine_cos = jnp.where(jnp.abs(fine_cos) < 1e-6, 1e-6, fine_cos)
    return jnp.cos(coarse), jnp.sin(coarse), fine_cos * SCALE, jnp.sin(fine) / fine_cos


def fill(step_tables, slab, c_buf, d_buf, hi_ref, lo_ref, at, rows):
    coarse_cos, coarse_sin, fine_cos, fine_tan = step_tables
    for lane in range(0, slab, LANE):
        highs, lows = ([], []), ([], [])
        for row in range(rows.start, rows.stop, 32):
            weight = c_buf[row : row + 32, lane : lane + LANE].astype(F32)
            delay = d_buf[row : row + 32, lane : lane + LANE]
            values = ([], [])
            for sub in range(0, 32, SUB):
                bins = delay[sub : sub + SUB]
                low, high = bins & (FINE - 1), bins >> 3
                cos_l, tan_l = gather_rows(fine_cos, low), gather_rows(fine_tan, low)
                cos_h, sin_h = gather_rows(coarse_cos, high), gather_rows(coarse_sin, high)
                size = weight[sub : sub + SUB] * cos_l
                values[0].append(size * (cos_h - sin_h * tan_l))
                values[1].append(size * (sin_h + cos_h * tan_l))
            for plane in range(2):
                value = jnp.concatenate(values[plane], axis=0)
                hi = value.astype(HIGH)
                highs[plane].append(hi)
                lows[plane].append((value - hi.astype(F32)).astype(LOW))
        to = pl.ds(pl.multiple_of(at + lane, LANE), LANE)
        for plane in range(2):
            hi_ref[plane, to, rows] = jnp.concatenate(highs[plane], axis=0).T
            lo_ref[plane, to, rows] = jnp.concatenate(lows[plane], axis=0).T


def multiply(left_c, left_s, hi_ref, lo_ref, here, rows):
    total = None
    for plane, left in ((0, left_c), (1, left_s)):
        for matrix in (hi_ref, lo_ref):
            part = jnp.dot(left[:, here], matrix[plane, here, rows], preferred_element_type=F32)
            total = part if total is None else total + part
    return total


def split(value):
    first = value.astype(HIGH).astype(F32)
    second = (value - first).astype(HIGH).astype(F32)
    third = (value - first - second).astype(HIGH).astype(F32)
    return first, second, third


def prepare(z_ref, left_c, left_s):
    peers, _, own = z_ref.shape
    whole = z_ref[0] * z_ref[0]
    for peer in range(1, peers):
        whole = whole + z_ref[peer] * z_ref[peer]
    squares = jnp.sum(jnp.sum(whole, axis=1, keepdims=True), axis=0, keepdims=True)
    inverse = 1.0 / jnp.sqrt(squares / (peers * own) + EPS)
    for peer in range(peers):
        here = slice(peer * own, (peer + 1) * own)
        normed = z_ref[peer] * inverse
        turned = jnp.concatenate([-normed[1:2], normed[0:1]], axis=0)
        for left, value in ((left_c, -normed), (left_s, turned)):
            pad = jnp.zeros((16 - 6, own), F32)
            left[:, here] = jnp.concatenate([*split(value), pad], axis=0).astype(HIGH)
    mine = z_ref[lax.axis_index("rows")] * inverse
    return mine, jnp.concatenate([-mine[1:2], mine[0:1]], axis=0)


def complete(step_count, totals, turned):
    product = (totals[0:2] + totals[2:4] + totals[4:6]) * (1.0 / SCALE)
    return product + step_count.astype(F32) * (math.pi / FTOTAL) * turned


def advance(chunk, step_count, z_ref, hi_ref, lo_ref, left_c, left_s):
    mine, turned = prepare(z_ref, left_c, left_s)
    nodes, own = hi_ref.shape[1:]

    def step(at, totals):
        here = pl.ds(pl.multiple_of(at * chunk, chunk), chunk)
        return totals + multiply(left_c, left_s, hi_ref, lo_ref, here, slice(0, own))

    totals = lax.fori_loop(0, nodes // chunk, step, jnp.zeros((16, own), F32))
    return mine, turned, complete(step_count, totals, turned)


def first_kernel(slab, q_ref, z_hbm, c_hbm, d_hbm, hi_ref, lo_ref, out_ref, z_buf, left_c, left_s, total, c_buf, d_buf, z_sem, c_sem, d_sem):
    own, nodes = c_hbm.shape
    slots = c_buf.shape[0]
    slabs = nodes // slab

    def copies(at, slot):
        here = pl.ds(pl.multiple_of(at * slab, slab), slab)
        return (
            pltpu.make_async_copy(c_hbm.at[:, here], c_buf.at[slot], c_sem.at[slot]),
            pltpu.make_async_copy(d_hbm.at[:, here], d_buf.at[slot], d_sem.at[slot]),
        )

    fetch = pltpu.make_async_copy(z_hbm, z_buf, z_sem)
    fetch.start()
    for at in range(min(slots - 1, slabs)):
        for copy in copies(at, at):
            copy.start()
    step_count = q_ref[0] + 1
    step_tables = tables(step_count)
    fetch.wait()
    _, turned = prepare(z_buf, left_c, left_s)
    total[...] = jnp.zeros_like(total)
    block = min(256, own)

    def body(at, carry):
        slot = lax.rem(at, slots)
        for copy in copies(at, slot):
            copy.wait()

        @pl.when(at + slots - 1 < slabs)
        def _():
            for copy in copies(at + slots - 1, lax.rem(at + slots - 1, slots)):
                copy.start()

        here = pl.ds(pl.multiple_of(at * slab, slab), slab)
        for row in range(0, own, block):
            rows = slice(row, row + block)
            fill(step_tables, slab, c_buf.at[slot], d_buf.at[slot], hi_ref, lo_ref, at * slab, rows)
            total[:, rows] += multiply(left_c, left_s, hi_ref, lo_ref, here, rows)
        return carry

    lax.fori_loop(0, slabs, body, 0)
    new = complete(step_count, total[...], turned)
    for peer in range(out_ref.shape[0]):
        out_ref[peer] = new


def next_kernel(chunk, q_ref, z_ref, hi_ref, lo_ref, out_ref, left_c, left_s):
    _, _, new = advance(chunk, q_ref[0] + 1, z_ref, hi_ref, lo_ref, left_c, left_s)
    for peer in range(out_ref.shape[0]):
        out_ref[peer] = new


def last_kernel(chunk, q_ref, z_ref, hi_ref, lo_ref, out_ref, sums_ref, left_c, left_s):
    mine, turned, new = advance(chunk, q_ref[0] + 1, z_ref, hi_ref, lo_ref, left_c, left_s)
    out_ref[...] = new

    def summed(value):
        return jnp.sum(jnp.sum(value, axis=1, keepdims=True), axis=0, keepdims=True)

    row = lax.broadcasted_iota(jnp.int32, (SUB, LANE), 0)
    sums = jnp.where(row == 0, summed(new * new), 0.0)
    sums = sums + jnp.where(row == 1, summed(mine * new), 0.0)
    sums = sums + jnp.where(row == 2, summed(turned * new), 0.0)
    for peer in range(sums_ref.shape[0]):
        sums_ref[peer] = sums


def first(step, z, coupling, delays):
    own, nodes = coupling.shape
    slab, slots = min(SLAB, nodes), 2
    shape = (2, nodes, own)
    return pl.pallas_call(
        functools.partial(first_kernel, slab),
        out_shape=(
            pltpu.VMEM(shape, HIGH),
            pltpu.VMEM(shape, LOW),
            pltpu.VMEM(z.shape, F32),
        ),
        in_specs=[SMEM, ANY, ANY, ANY],
        out_specs=(VMEM, VMEM, VMEM),
        scratch_shapes=[
            pltpu.VMEM(z.shape, F32),
            pltpu.VMEM((16, nodes), HIGH),
            pltpu.VMEM((16, nodes), HIGH),
            pltpu.VMEM((16, own), F32),
            pltpu.VMEM((slots, own, slab), coupling.dtype),
            pltpu.VMEM((slots, own, slab), delays.dtype),
            pltpu.SemaphoreType.DMA,
            pltpu.SemaphoreType.DMA((slots,)),
            pltpu.SemaphoreType.DMA((slots,)),
        ],
        compiler_params=pltpu.CompilerParams(vmem_limit_bytes=GRANT),
        name="first",
    )(step, z, coupling, delays)


def apply(kernel, outputs, step, z, hi, lo):
    nodes = z.shape[0] * z.shape[2]
    return pl.pallas_call(
        functools.partial(kernel, min(CHUNK, nodes)),
        out_shape=tuple(pltpu.VMEM(shape, F32) for shape in outputs),
        in_specs=[SMEM, VMEM, VMEM, VMEM],
        out_specs=(VMEM,) * len(outputs),
        scratch_shapes=[pltpu.VMEM((16, nodes), HIGH), pltpu.VMEM((16, nodes), HIGH)],
        compiler_params=pltpu.CompilerParams(vmem_limit_bytes=GRANT),
        name="apply",
    )(step, z, hi, lo)


def finish_kernel(nodes, y_ref, sums_ref, vector_ref, value_ref):
    sums = jnp.sum(sums_ref[...], axis=0)
    vector_ref[...] = y_ref[...] * (1.0 / jnp.sqrt(sums[0:1, 0:1] / nodes + EPS))
    lane = lax.broadcasted_iota(jnp.int32, (1, LANE), 1)
    value_ref[...] = jnp.where(lane == 0, sums[1:2], sums[2:3]) * (1.0 / nodes)


def finish(nodes, y, sums):
    return pl.pallas_call(
        functools.partial(finish_kernel, nodes),
        out_shape=(jax.ShapeDtypeStruct(y.shape, F32), jax.ShapeDtypeStruct((1, LANE), F32)),
        in_specs=[VMEM, VMEM],
        out_specs=(VMEM, VMEM),
        name="finish",
    )(y, sums)


def copies_of_all(value):
    return lax.all_to_all(value, "rows", 0, 0, tiled=True)


def exchange(value):
    return in_vmem(copies_of_all(value))


def in_vmem(value):
    return pltpu.with_memory_space_constraint(value, pltpu.VMEM)


def solution(mesh):
    peers = mesh.shape["rows"]

    def point(coupling, delays, step, start):
        nodes = coupling.shape[1]
        z = copies_of_all(jnp.broadcast_to(start[None], (peers, *start.shape)))
        hi, lo, y = first(step, z, coupling, delays)
        hi, lo = in_vmem(hi), in_vmem(lo)
        for sweep in range(1, ITERS - 1):
            (y,) = apply(next_kernel, [z.shape], step, exchange(y), hi, lo)
        y, sums = apply(last_kernel, [z.shape[1:], (peers, SUB, LANE)], step, exchange(y), hi, lo)
        return finish(nodes, y, exchange(sums))

    def shards(coupling, delays, freq_index, initial):
        vectors, values = [], []
        for at in range(freq_index.shape[0]):
            vector, value = point(coupling, delays, freq_index[at : at + 1], initial[at])
            vectors.append(vector)
            values.append(value[0, 0:2])
        return jnp.stack(vectors), jnp.stack(values)

    return jax.shard_map(
        shards,
        mesh=mesh,
        in_specs=(P("rows", None), P("rows", None), P("freq"), P("freq", None, "rows")),
        out_specs=(P("freq", None, "rows"), P("freq", None)),
        check_vma=False,
    )
```

time: 151 us -> 113 us (0.75)
  Pallas kernels: 96 us -> 64.1 us
  blocking collectives: 39.3 us -> 33 us
    pallas_call x3, Pallas kernels: 45.9 us -> 22.3 us  [apply(): pl.pallas_call(functools.partial(kernel, min(CHUNK, nodes)), out_shape=tu...]
    pallas_call x1, Pallas kernels: 48.7 us -> 40.5 us  [first(): pl.pallas_call(functools.partial(first_kernel, slab), out_shape=(pltpu.VM...]
    all_to_all x4, blocking collectives: 39.3 us -> 33 us  [copies_of_all(): return lax.all_to_all(value, 'rows', 0, 0, tiled=True)]
where the time goes in v2:
time: 113 us; the launch traced here: 112 us
  Pallas kernels  64.1 us (57%)
  blocking collectives  33 us (29%)
  starting transfers between devices  6.35 us (6%)
  waiting for transfers between devices  5.27 us (5%)
  local copies, waits for them, and re-layouts  1.98 us (2%)
  between operations  1.32 us (1%)
    pallas_call x1, Pallas kernels, first(): pl.pallas_call(functools.partial(first_kernel, slab), out_shape=(pltpu.VM...  40.5 us
    all_to_all x4, blocking collectives, copies_of_all(): return lax.all_to_all(value, 'rows', 0, 0, tiled=True)  33 us
    pallas_call x3, Pallas kernels, apply(): pl.pallas_call(functools.partial(kernel, min(CHUNK, nodes)), out_shape=tu...  22.3 us
    all_to_all x1, starting transfers between devices, copies_of_all(): return lax.all_to_all(value, 'rows', 0, 0, tiled=True)  6.35 us
    all_to_all x1, waiting for transfers between devices, copies_of_all(): return lax.all_to_all(value, 'rows', 0, 0, tiled=True)  5.27 us
  transfers between devices with their start and end apart: 1, of which 1 were waited for; matrix products, arithmetic and copies ran while one was open for 0% of the time, Pallas kernels for 0%

profile of v2, /device:TPU:0, one launch (start us, length us, event | category | flops | bytes accessed | tf_op | source)
XLA Modules:
  0.0 112.1 jit_solution(7239783556769129967)
XLA Ops:
  0.6 1.3 %broadcast_in_dim.8 = f32[8,2,1024]{2,1,0:T(2,128)} broadcast(f32[2,1024]{1,0:T(2,128)} %bitcast.3), dimensions={1,2} | broadcast | bytes 73728 | tf_op jit(solution)/shard_map/broadcast_in_dim | solution.py:280
  2.0 6.4 %all-to-all-start = ((f32[8,2,1024]{2,1,0:T(2,128)}), f32[8,2,1024]{2,1,0:T(2,128)S(1)}, u32[]{:S(2)}, u32[]{:S(2)}) async-start(f32[8,2,1024]{2,1,0:T(2,128)} %broadcast_in_dim.8), calls=%async_computation | async-start | bytes 131072 | tf_op jit(solution)/shard_map/all_to_all | solution.py:264
  9.0 5.3 %all-to-all-done.z_hbm = f32[8,2,1024]{2,1,0:T(2,128)S(1)} async-done(((f32[8,2,1024]{2,1,0:T(2,128)}), f32[8,2,1024]{2,1,0:T(2,128)S(1)}, u32[]{:S(2)}, u32[]{:S(2)}) %all-to-all-start) | async-done | bytes 65568 | tf_op jit(solution)/shard_map/all_to_all | solution.py:264
  14.2 0.0 copy-start.1
  14.2 0.6 copy-done.1
  14.9 40.5 %first.1 = (bf16[2,8192,1024]{2,1,0:T(8,128)(2,1)S(1)}, f8e4m3fn[2,8192,1024]{2,1,0:T(32,128)(4,1)S(1)}, f32[8,2,1024]{2,1,0:T(2,128)S(1)}) custom-call(s32[1]{0:T(128)S(6)} %copy.6.q_ref, f32[8,2,1024]{2,1,0:T(2,128)} %copy-done.1, bf16[1024,8192]{1,0:T(8,128)(2,1)} %c_hbm.1, s32[1024,8192]{1,0:T(8,128)} %d_hbm.1), custom_call_target="tpu_custom_call" | custom-call | tf_op jit(solution)/shard_map/first/pallas_call | solution.py:208
  55.3 8.3 %all_to_all.25.z_ref = f32[8,2,1024]{2,1,0:T(2,128)S(1)} all-to-all(f32[8,2,1024]{2,1,0:T(2,128)S(1)} %get-tuple-element.9), channel_id=1, replica_groups=mesh['freq'=4,'rows'=8] {'rows'}, dimensions={0} | all-to-all | bytes 131072 | tf_op jit(solution)/shard_map/all_to_all | solution.py:264
  63.6 7.4 %apply.3 = f32[8,2,1024]{2,1,0:T(2,128)S(1)} custom-call(s32[1]{0:T(128)S(6)} %copy.6.q_ref, f32[8,2,1024]{2,1,0:T(2,128)S(1)} %all_to_all.25.z_ref, bf16[2,8192,1024]{2,1,0:T(8,128)(2,1)S(1)} %get-tuple-element.10.hi_ref, f8e4m3fn[2,8192,1024]{2,1,0:T(32,128)(4,1)S(1)} %get-tuple-element.11.lo_ref), custom_call_target="tpu_custom_call" | custom-call | tf_op jit(solution)/shard_map/apply/pallas_call | solution.py:235
  71.1 8.3 %all_to_all.26.z_ref = f32[8,2,1024]{2,1,0:T(2,128)S(1)} all-to-all(f32[8,2,1024]{2,1,0:T(2,128)S(1)} %apply.3), channel_id=1, replica_groups=mesh['freq'=4,'rows'=8] {'rows'}, dimensions={0} | all-to-all | bytes 131072 | tf_op jit(solution)/shard_map/all_to_all | solution.py:264
  79.4 7.4 %apply.4 = f32[8,2,1024]{2,1,0:T(2,128)S(1)} custom-call(s32[1]{0:T(128)S(6)} %copy.6.q_ref, f32[8,2,1024]{2,1,0:T(2,128)S(1)} %all_to_all.26.z_ref, bf16[2,8192,1024]{2,1,0:T(8,128)(2,1)S(1)} %get-tuple-element.10.hi_ref, f8e4m3fn[2,8192,1024]{2,1,0:T(32,128)(4,1)S(1)} %get-tuple-element.11.lo_ref), custom_call_target="tpu_custom_call" | custom-call | tf_op jit(solution)/shard_map/apply/pallas_call | solution.py:235
  86.8 8.3 %all_to_all.27.z_ref = f32[8,2,1024]{2,1,0:T(2,128)S(1)} all-to-all(f32[8,2,1024]{2,1,0:T(2,128)S(1)} %apply.4), channel_id=1, replica_groups=mesh['freq'=4,'rows'=8] {'rows'}, dimensions={0} | all-to-all | bytes 131072 | tf_op jit(solution)/shard_map/all_to_all | solution.py:264
  95.1 7.5 %apply.5 = (f32[2,1024]{1,0:T(2,128)S(1)}, f32[8,8,128]{2,1,0:T(8,128)S(1)}) custom-call(s32[1]{0:T(128)S(6)} %copy.6.q_ref, f32[8,2,1024]{2,1,0:T(2,128)S(1)} %all_to_all.27.z_ref, bf16[2,8192,1024]{2,1,0:T(8,128)(2,1)S(1)} %get-tuple-element.10.hi_ref, f8e4m3fn[2,8192,1024]{2,1,0:T(32,128)(4,1)S(1)} %get-tuple-element.11.lo_ref), custom_call_target="tpu_custom_call" | custom-call | tf_op jit(solution)/shard_map/apply/pallas_call | solution.py:235
  102.6 0.0 copy-start
  102.6 8.1 %all_to_all.28.sums_ref = f32[8,8,128]{2,1,0:T(8,128)S(1)} all-to-all(f32[8,8,128]{2,1,0:T(8,128)S(1)} %get-tuple-element.13), channel_id=1, replica_groups=mesh['freq'=4,'rows'=8] {'rows'}, dimensions={0} | all-to-all | bytes 65536 | tf_op jit(solution)/shard_map/all_to_all | solution.py:264
  110.7 0.0 copy-done
  110.7 1.4 %finish.1 = (f32[2,1024]{1,0:T(2,128)}, f32[1,128]{1,0:T(1,128)}) custom-call(f32[2,1024]{1,0:T(2,128)} %copy-done, f32[8,8,128]{2,1,0:T(8,128)S(1)} %all_to_all.28.sums_ref), custom_call_target="tpu_custom_call" | custom-call | tf_op jit(solution)/shard_map/finish/pallas_call | solution.py:254
Async XLA Ops:
  2.0 12.3 %all-to-all-start = ((f32[8,2,1024]{2,1,0:T(2,128)}), f32[8,2,1024]{2,1,0:T(2,128)S(1)}, u32[]{:S(2)}, u32[]{:S(2)}) async-start(f32[8,2,1024]{2,1,0:T(2,128)} %broadcast_in_dim.8), calls=%async_computation | async-start | bytes 131072 | tf_op jit(solution)/shard_map/all_to_all | solution.py:264
  14.2 0.6 copy-start.1
  102.6 8.1 %copy-start = (f32[2,1024]{1,0:T(2,128)}, f32[2,1024]{1,0:T(2,128)S(1)}, u32[]{:S(2)}) copy-start(f32[2,1024]{1,0:T(2,128)S(1)} %get-tuple-element.12.y_ref) | copy-start | bytes 24580

commit v3 on v2

--- a/solution.py
+++ b/solution.py
@@ -55,38 +55,42 @@
     return jnp.cos(coarse), jnp.sin(coarse), fine_cos * SCALE, jnp.sin(fine) / fine_cos
 
 
-def fill(step_tables, slab, c_buf, d_buf, hi_ref, lo_ref, at, rows):
-    coarse_cos, coarse_sin, fine_cos, fine_tan = step_tables
+def fill(table_ref, slab, c_buf, d_buf, hi_ref, lo_ref, at, rows):
     for lane in range(0, slab, LANE):
-        highs, lows = ([], []), ([], [])
-        for row in range(rows.start, rows.stop, 32):
-            weight = c_buf[row : row + 32, lane : lane + LANE].astype(F32)
-            delay = d_buf[row : row + 32, lane : lane + LANE]
-            values = ([], [])
-            for sub in range(0, 32, SUB):
-                bins = delay[sub : sub + SUB]
-                low, high = bins & (FINE - 1), bins >> 3
-                cos_l, tan_l = gather_rows(fine_cos, low), gather_rows(fine_tan, low)
-                cos_h, sin_h = gather_rows(coarse_cos, high), gather_rows(coarse_sin, high)
-                size = weight[sub : sub + SUB] * cos_l
-                values[0].append(size * (cos_h - sin_h * tan_l))
-                values[1].append(size * (sin_h + cos_h * tan_l))
-            for plane in range(2):
-                value = jnp.concatenate(values[plane], axis=0)
-                hi = value.astype(HIGH)
-                highs[plane].append(hi)
-                lows[plane].append((value - hi.astype(F32)).astype(LOW))
-        to = pl.ds(pl.multiple_of(at + lane, LANE), LANE)
+        for row in range(rows.start, rows.stop, LANE):
+            fill_block(table_ref, c_buf, d_buf, hi_ref, lo_ref, at, lane, row)
+
+
+def fill_block(table_ref, c_buf, d_buf, hi_ref, lo_ref, at, lane, row):
+    coarse_cos, coarse_sin, fine_cos, fine_tan = (table_ref[i] for i in range(4))
+    rows, lanes = slice(row, row + LANE), slice(lane, lane + LANE)
+    weights = c_buf[rows, lanes].T.astype(F32)
+    delays = d_buf[rows, lanes].T
+    for first in range(0, LANE, 32):
+        values = ([], [])
+        for sub in range(first, first + 32, SUB):
+            bins = delays[sub : sub + SUB]
+            low, high = bins & (FINE - 1), bins >> 3
+            cos_l, tan_l = gather_rows(fine_cos, low), gather_rows(fine_tan, low)
+            cos_h, sin_h = gather_rows(coarse_cos, high), gather_rows(coarse_sin, high)
+            size = weights[sub : sub + SUB] * cos_l
+            values[0].append(size * (cos_h - sin_h * tan_l))
+            values[1].append(size * (sin_h + cos_h * tan_l))
+        to = pl.ds(pl.multiple_of(at + lane + first, 32), 32)
         for plane in range(2):
-            hi_ref[plane, to, rows] = jnp.concatenate(highs[plane], axis=0).T
-            lo_ref[plane, to, rows] = jnp.concatenate(lows[plane], axis=0).T
+            value = jnp.concatenate(values[plane], axis=0)
+            hi = value.astype(HIGH)
+            hi_ref[plane, row // LANE, to, :] = hi
+            lo_ref[plane, to, rows] = (value - hi.astype(F32)).astype(LOW)
 
 
 def multiply(left_c, left_s, hi_ref, lo_ref, here, rows):
     total = None
     for plane, left in ((0, left_c), (1, left_s)):
-        for matrix in (hi_ref, lo_ref):
-            part = jnp.dot(left[:, here], matrix[plane, here, rows], preferred_element_type=F32)
+        blocks = range(rows.start // LANE, rows.stop // LANE)
+        high = jnp.concatenate([hi_ref[plane, block, here] for block in blocks], axis=1)
+        for matrix in (high, lo_ref[plane, here, rows]):
+            part = jnp.dot(left[:, here], matrix, preferred_element_type=F32)
             total = part if total is None else total + part
     return total
 
@@ -123,7 +127,7 @@
 
 def advance(chunk, step_count, z_ref, hi_ref, lo_ref, left_c, left_s):
     mine, turned = prepare(z_ref, left_c, left_s)
-    nodes, own = hi_ref.shape[1:]
+    nodes, own = lo_ref.shape[1:]
 
     def step(at, totals):
         here = pl.ds(pl.multiple_of(at * chunk, chunk), chunk)
@@ -133,7 +137,7 @@
     return mine, turned, complete(step_count, totals, turned)
 
 
-def first_kernel(slab, q_ref, z_hbm, c_hbm, d_hbm, hi_ref, lo_ref, out_ref, z_buf, left_c, left_s, total, c_buf, d_buf, z_sem, c_sem, d_sem):
+def first_kernel(slab, q_ref, z_hbm, c_hbm, d_hbm, hi_ref, lo_ref, out_ref, z_buf, left_c, left_s, total, table_ref, c_buf, d_buf, z_sem, c_sem, d_sem):
     own, nodes = c_hbm.shape
     slots = c_buf.shape[0]
     slabs = nodes // slab
@@ -151,7 +155,8 @@
         for copy in copies(at, at):
             copy.start()
     step_count = q_ref[0] + 1
-    step_tables = tables(step_count)
+    for at, table in enumerate(tables(step_count)):
+        table_ref[at] = table
     fetch.wait()
     _, turned = prepare(z_buf, left_c, left_s)
     total[...] = jnp.zeros_like(total)
@@ -170,7 +175,7 @@
         here = pl.ds(pl.multiple_of(at * slab, slab), slab)
         for row in range(0, own, block):
             rows = slice(row, row + block)
-            fill(step_tables, slab, c_buf.at[slot], d_buf.at[slot], hi_ref, lo_ref, at * slab, rows)
+            fill(table_ref, slab, c_buf.at[slot], d_buf.at[slot], hi_ref, lo_ref, at * slab, rows)
             total[:, rows] += multiply(left_c, left_s, hi_ref, lo_ref, here, rows)
         return carry
 
@@ -204,12 +209,11 @@
 def first(step, z, coupling, delays):
     own, nodes = coupling.shape
     slab, slots = min(SLAB, nodes), 2
-    shape = (2, nodes, own)
     return pl.pallas_call(
         functools.partial(first_kernel, slab),
         out_shape=(
-            pltpu.VMEM(shape, HIGH),
-            pltpu.VMEM(shape, LOW),
+            pltpu.VMEM((2, own // LANE, nodes, LANE), HIGH),
+            pltpu.VMEM((2, nodes, own), LOW),
             pltpu.VMEM(z.shape, F32),
         ),
         in_specs=[SMEM, ANY, ANY, ANY],
@@ -219,6 +223,7 @@
             pltpu.VMEM((16, nodes), HIGH),
             pltpu.VMEM((16, nodes), HIGH),
             pltpu.VMEM((16, own), F32),
+            pltpu.VMEM((4, SUB, LANE), F32),
             pltpu.VMEM((slots, own, slab), coupling.dtype),
             pltpu.VMEM((slots, own, slab), delays.dtype),
             pltpu.SemaphoreType.DMA,

time: 113 us -> 107 us (0.947)
  Pallas kernels: 64.1 us -> 58.4 us
    pallas_call x1, Pallas kernels: 40.5 us -> 34.8 us  [first(): pl.pallas_call(functools.partial(first_kernel, slab), out_shape=(pltpu.VM...]
where the time goes in v3:
time: 107 us; the launch traced here: 106 us
  Pallas kernels  58.4 us (55%)
  blocking collectives  33 us (31%)
  starting transfers between devices  6.35 us (6%)
  waiting for transfers between devices  5.27 us (5%)
  local copies, waits for them, and re-layouts  1.98 us (2%)
  between operations  1.32 us (1%)
    pallas_call x1, Pallas kernels, first(): pl.pallas_call(functools.partial(first_kernel, slab), out_shape=(pltpu.VM...  34.8 us
    all_to_all x4, blocking collectives, copies_of_all(): return lax.all_to_all(value, 'rows', 0, 0, tiled=True)  33 us
    pallas_call x3, Pallas kernels, apply(): pl.pallas_call(functools.partial(kernel, min(CHUNK, nodes)), out_shape=tu...  22.3 us
    all_to_all x1, starting transfers between devices, copies_of_all(): return lax.all_to_all(value, 'rows', 0, 0, tiled=True)  6.35 us
    all_to_all x1, waiting for transfers between devices, copies_of_all(): return lax.all_to_all(value, 'rows', 0, 0, tiled=True)  5.27 us
  transfers between devices with their start and end apart: 1, of which 1 were waited for; matrix products, arithmetic and copies ran while one was open for 0% of the time, Pallas kernels for 0%

profile of v3, /device:TPU:0, one launch (start us, length us, event | category | flops | bytes accessed | tf_op | source)
XLA Modules:
  0.0 106.4 jit_solution(2041262649545563407)
XLA Ops:
  0.6 1.3 %broadcast_in_dim.8 = f32[8,2,1024]{2,1,0:T(2,128)} broadcast(f32[2,1024]{1,0:T(2,128)} %bitcast.3), dimensions={1,2} | broadcast | bytes 73728 | tf_op jit(solution)/shard_map/broadcast_in_dim | solution.py:285
  2.0 6.4 %all-to-all-start = ((f32[8,2,1024]{2,1,0:T(2,128)}), f32[8,2,1024]{2,1,0:T(2,128)S(1)}, u32[]{:S(2)}, u32[]{:S(2)}) async-start(f32[8,2,1024]{2,1,0:T(2,128)} %broadcast_in_dim.8), calls=%async_computation | async-start | bytes 131072 | tf_op jit(solution)/shard_map/all_to_all | solution.py:269
  9.0 5.3 %all-to-all-done.z_hbm = f32[8,2,1024]{2,1,0:T(2,128)S(1)} async-done(((f32[8,2,1024]{2,1,0:T(2,128)}), f32[8,2,1024]{2,1,0:T(2,128)S(1)}, u32[]{:S(2)}, u32[]{:S(2)}) %all-to-all-start) | async-done | bytes 65568 | tf_op jit(solution)/shard_map/all_to_all | solution.py:269
  14.2 0.0 copy-start.1
  14.2 0.6 copy-done.1
  14.9 34.8 %first.1 = (bf16[2,8,8192,128]{3,2,1,0:T(8,128)(2,1)S(1)}, f8e4m3fn[2,8192,1024]{2,1,0:T(32,128)(4,1)S(1)}, f32[8,2,1024]{2,1,0:T(2,128)S(1)}) custom-call(s32[1]{0:T(128)S(6)} %copy.6.q_ref, f32[8,2,1024]{2,1,0:T(2,128)} %copy-done.1, bf16[1024,8192]{1,0:T(8,128)(2,1)} %c_hbm.1, s32[1024,8192]{1,0:T(8,128)} %d_hbm.1), custom_call_target="tpu_custom_call" | custom-call | tf_op jit(solution)/shard_map/first/pallas_call | solution.py:212
  49.6 8.3 %all_to_all.25.z_ref = f32[8,2,1024]{2,1,0:T(2,128)S(1)} all-to-all(f32[8,2,1024]{2,1,0:T(2,128)S(1)} %get-tuple-element.9), channel_id=1, replica_groups=mesh['freq'=4,'rows'=8] {'rows'}, dimensions={0} | all-to-all | bytes 131072 | tf_op jit(solution)/shard_map/all_to_all | solution.py:269
  57.9 7.4 %apply.3 = f32[8,2,1024]{2,1,0:T(2,128)S(1)} custom-call(s32[1]{0:T(128)S(6)} %copy.6.q_ref, f32[8,2,1024]{2,1,0:T(2,128)S(1)} %all_to_all.25.z_ref, bf16[2,8,8192,128]{3,2,1,0:T(8,128)(2,1)S(1)} %get-tuple-element.10.hi_ref, f8e4m3fn[2,8192,1024]{2,1,0:T(32,128)(4,1)S(1)} %get-tuple-element.11.lo_ref), custom_call_target="tpu_custom_call" | custom-call | tf_op jit(solution)/shard_map/apply/pallas_call | solution.py:240
  65.4 8.3 %all_to_all.26.z_ref = f32[8,2,1024]{2,1,0:T(2,128)S(1)} all-to-all(f32[8,2,1024]{2,1,0:T(2,128)S(1)} %apply.3), channel_id=1, replica_groups=mesh['freq'=4,'rows'=8] {'rows'}, dimensions={0} | all-to-all | bytes 131072 | tf_op jit(solution)/shard_map/all_to_all | solution.py:269
  73.7 7.4 %apply.4 = f32[8,2,1024]{2,1,0:T(2,128)S(1)} custom-call(s32[1]{0:T(128)S(6)} %copy.6.q_ref, f32[8,2,1024]{2,1,0:T(2,128)S(1)} %all_to_all.26.z_ref, bf16[2,8,8192,128]{3,2,1,0:T(8,128)(2,1)S(1)} %get-tuple-element.10.hi_ref, f8e4m3fn[2,8192,1024]{2,1,0:T(32,128)(4,1)S(1)} %get-tuple-element.11.lo_ref), custom_call_target="tpu_custom_call" | custom-call | tf_op jit(solution)/shard_map/apply/pallas_call | solution.py:240
  81.1 8.3 %all_to_all.27.z_ref = f32[8,2,1024]{2,1,0:T(2,128)S(1)} all-to-all(f32[8,2,1024]{2,1,0:T(2,128)S(1)} %apply.4), channel_id=1, replica_groups=mesh['freq'=4,'rows'=8] {'rows'}, dimensions={0} | all-to-all | bytes 131072 | tf_op jit(solution)/shard_map/all_to_all | solution.py:269
  89.4 7.5 %apply.5 = (f32[2,1024]{1,0:T(2,128)S(1)}, f32[8,8,128]{2,1,0:T(8,128)S(1)}) custom-call(s32[1]{0:T(128)S(6)} %copy.6.q_ref, f32[8,2,1024]{2,1,0:T(2,128)S(1)} %all_to_all.27.z_ref, bf16[2,8,8192,128]{3,2,1,0:T(8,128)(2,1)S(1)} %get-tuple-element.10.hi_ref, f8e4m3fn[2,8192,1024]{2,1,0:T(32,128)(4,1)S(1)} %get-tuple-element.11.lo_ref), custom_call_target="tpu_custom_call" | custom-call | tf_op jit(solution)/shard_map/apply/pallas_call | solution.py:240
  96.9 0.0 copy-start
  96.9 8.1 %all_to_all.28.sums_ref = f32[8,8,128]{2,1,0:T(8,128)S(1)} all-to-all(f32[8,8,128]{2,1,0:T(8,128)S(1)} %get-tuple-element.13), channel_id=1, replica_groups=mesh['freq'=4,'rows'=8] {'rows'}, dimensions={0} | all-to-all | bytes 65536 | tf_op jit(solution)/shard_map/all_to_all | solution.py:269
  105.0 0.0 copy-done
  105.0 1.4 %finish.1 = (f32[2,1024]{1,0:T(2,128)}, f32[1,128]{1,0:T(1,128)}) custom-call(f32[2,1024]{1,0:T(2,128)} %copy-done, f32[8,8,128]{2,1,0:T(8,128)S(1)} %all_to_all.28.sums_ref), custom_call_target="tpu_custom_call" | custom-call | tf_op jit(solution)/shard_map/finish/pallas_call | solution.py:259
Async XLA Ops:
  2.0 12.3 %all-to-all-start = ((f32[8,2,1024]{2,1,0:T(2,128)}), f32[8,2,1024]{2,1,0:T(2,128)S(1)}, u32[]{:S(2)}, u32[]{:S(2)}) async-start(f32[8,2,1024]{2,1,0:T(2,128)} %broadcast_in_dim.8), calls=%async_computation | async-start | bytes 131072 | tf_op jit(solution)/shard_map/all_to_all | solution.py:269
  14.2 0.6 copy-start.1
  96.9 8.1 %copy-start = (f32[2,1024]{1,0:T(2,128)}, f32[2,1024]{1,0:T(2,128)S(1)}, u32[]{:S(2)}) copy-start(f32[2,1024]{1,0:T(2,128)S(1)} %get-tuple-element.12.y_ref) | copy-start | bytes 24580

commit v4 on v3

--- a/solution.py
+++ b/solution.py
@@ -20,8 +20,8 @@
 SMEM = pl.BlockSpec(memory_space=pltpu.SMEM)
 ANY = pl.BlockSpec(memory_space=pl.ANY)
 SUB, LANE, FINE = 8, 128, 8
-GRANT = 8 * 2**20
-CHUNK = 2048
+GRANT = 17 * 2**19
+CHUNK = 4096
 SLAB = 512
 
 
@@ -137,7 +137,7 @@
     return mine, turned, complete(step_count, totals, turned)
 
 
-def first_kernel(slab, q_ref, z_hbm, c_hbm, d_hbm, hi_ref, lo_ref, out_ref, z_buf, left_c, left_s, total, table_ref, c_buf, d_buf, z_sem, c_sem, d_sem):
+def first_kernel(slab, q_ref, z_ref, c_hbm, d_hbm, hi_ref, lo_ref, out_ref, left_c, left_s, total, table_ref, c_buf, d_buf, c_sem, d_sem):
     own, nodes = c_hbm.shape
     slots = c_buf.shape[0]
     slabs = nodes // slab
@@ -149,16 +149,13 @@
             pltpu.make_async_copy(d_hbm.at[:, here], d_buf.at[slot], d_sem.at[slot]),
         )
 
-    fetch = pltpu.make_async_copy(z_hbm, z_buf, z_sem)
-    fetch.start()
     for at in range(min(slots - 1, slabs)):
         for copy in copies(at, at):
             copy.start()
     step_count = q_ref[0] + 1
     for at, table in enumerate(tables(step_count)):
         table_ref[at] = table
-    fetch.wait()
-    _, turned = prepare(z_buf, left_c, left_s)
+    _, turned = prepare(z_ref, left_c, left_s)
     total[...] = jnp.zeros_like(total)
     block = min(256, own)
 
@@ -216,21 +213,19 @@
             pltpu.VMEM((2, nodes, own), LOW),
             pltpu.VMEM(z.shape, F32),
         ),
-        in_specs=[SMEM, ANY, ANY, ANY],
+        in_specs=[SMEM, VMEM, ANY, ANY],
         out_specs=(VMEM, VMEM, VMEM),
         scratch_shapes=[
-            pltpu.VMEM(z.shape, F32),
             pltpu.VMEM((16, nodes), HIGH),
             pltpu.VMEM((16, nodes), HIGH),
             pltpu.VMEM((16, own), F32),
             pltpu.VMEM((4, SUB, LANE), F32),
             pltpu.VMEM((slots, own, slab), coupling.dtype),
             pltpu.VMEM((slots, own, slab), delays.dtype),
-            pltpu.SemaphoreType.DMA,
             pltpu.SemaphoreType.DMA((slots,)),
             pltpu.SemaphoreType.DMA((slots,)),
         ],
-        compiler_params=pltpu.CompilerParams(vmem_limit_bytes=GRANT),
+        compiler_params=pltpu.CompilerParams(vmem_limit_bytes=GRANT - 4 * math.prod(z.shape)),
         name="first",
     )(step, z, coupling, delays)
 
@@ -282,7 +277,7 @@
 
     def point(coupling, delays, step, start):
         nodes = coupling.shape[1]
-        z = copies_of_all(jnp.broadcast_to(start[None], (peers, *start.shape)))
+        z = exchange(jnp.broadcast_to(start[None], (peers, *start.shape)))
         hi, lo, y = first(step, z, coupling, delays)
         hi, lo = in_vmem(hi), in_vmem(lo)
         for sweep in range(1, ITERS - 1):

time: 107 us -> 105 us (0.981)
  no operation moved by 1% of the time
where the time goes in v4:
time: 105 us
  Pallas kernels  57.7 us (55%)
  blocking collectives  33 us (31%)
  starting transfers between devices  6.35 us (6%)
  waiting for transfers between devices  5.27 us (5%)
  local copies, waits for them, and re-layouts  1.33 us (1%)
  between operations  1.32 us (1%)
    pallas_call x1, Pallas kernels, first(): pl.pallas_call(functools.partial(first_kernel, slab), out_shape=(pltpu.VM...  34.7 us
    all_to_all x4, blocking collectives, copies_of_all(): return lax.all_to_all(value, 'rows', 0, 0, tiled=True)  33 us
    pallas_call x3, Pallas kernels, apply(): pl.pallas_call(functools.partial(kernel, min(CHUNK, nodes)), out_shape=tu...  21.6 us
    all_to_all x1, starting transfers between devices, copies_of_all(): return lax.all_to_all(value, 'rows', 0, 0, tiled=True)  6.35 us
    all_to_all x1, waiting for transfers between devices, copies_of_all(): return lax.all_to_all(value, 'rows', 0, 0, tiled=True)  5.27 us
  transfers between devices with their start and end apart: 1, of which 1 were waited for; matrix products, arithmetic and copies ran while one was open for 0% of the time, Pallas kernels for 0%

profile of v4, /device:TPU:0, one launch (start us, length us, event | category | flops | bytes accessed | tf_op | source)
XLA Modules:
  0.0 105.0 jit_solution(5050527129270437521)
XLA Ops:
  0.6 1.3 %broadcast_in_dim.8 = f32[8,2,1024]{2,1,0:T(2,128)} broadcast(f32[2,1024]{1,0:T(2,128)} %bitcast.3), dimensions={1,2} | broadcast | bytes 73728 | tf_op jit(solution)/shard_map/broadcast_in_dim | solution.py:280
  2.0 6.4 %all-to-all-start = ((f32[8,2,1024]{2,1,0:T(2,128)}), f32[8,2,1024]{2,1,0:T(2,128)S(1)}, u32[]{:S(2)}, u32[]{:S(2)}) async-start(f32[8,2,1024]{2,1,0:T(2,128)} %broadcast_in_dim.8), calls=%async_computation | async-start | bytes 131072 | tf_op jit(solution)/shard_map/all_to_all | solution.py:264
  9.0 5.3 %all-to-all-done.z_ref = f32[8,2,1024]{2,1,0:T(2,128)S(1)} async-done(((f32[8,2,1024]{2,1,0:T(2,128)}), f32[8,2,1024]{2,1,0:T(2,128)S(1)}, u32[]{:S(2)}, u32[]{:S(2)}) %all-to-all-start) | async-done | bytes 65568 | tf_op jit(solution)/shard_map/all_to_all | solution.py:264
  14.2 34.7 %first.1 = (bf16[2,8,8192,128]{3,2,1,0:T(8,128)(2,1)S(1)}, f8e4m3fn[2,8192,1024]{2,1,0:T(32,128)(4,1)S(1)}, f32[8,2,1024]{2,1,0:T(2,128)S(1)}) custom-call(s32[1]{0:T(128)S(6)} %copy.6.q_ref, f32[8,2,1024]{2,1,0:T(2,128)S(1)} %all-to-all-done.z_ref, bf16[1024,8192]{1,0:T(8,128)(2,1)} %c_hbm.1, s32[1024,8192]{1,0:T(8,128)} %d_hbm.1), custom_call_target="tpu_custom_call" | custom-call | tf_op jit(solution)/shard_map/first/pallas_call | solution.py:209
  49.0 8.3 %all_to_all.25.z_ref = f32[8,2,1024]{2,1,0:T(2,128)S(1)} all-to-all(f32[8,2,1024]{2,1,0:T(2,128)S(1)} %get-tuple-element.9), channel_id=1, replica_groups=mesh['freq'=4,'rows'=8] {'rows'}, dimensions={0} | all-to-all | bytes 131072 | tf_op jit(solution)/shard_map/all_to_all | solution.py:264
  57.3 7.2 %apply.3 = f32[8,2,1024]{2,1,0:T(2,128)S(1)} custom-call(s32[1]{0:T(128)S(6)} %copy.6.q_ref, f32[8,2,1024]{2,1,0:T(2,128)S(1)} %all_to_all.25.z_ref, bf16[2,8,8192,128]{3,2,1,0:T(8,128)(2,1)S(1)} %get-tuple-element.10.hi_ref, f8e4m3fn[2,8192,1024]{2,1,0:T(32,128)(4,1)S(1)} %get-tuple-element.11.lo_ref), custom_call_target="tpu_custom_call" | custom-call | tf_op jit(solution)/shard_map/apply/pallas_call | solution.py:235
  64.4 8.3 %all_to_all.26.z_ref = f32[8,2,1024]{2,1,0:T(2,128)S(1)} all-to-all(f32[8,2,1024]{2,1,0:T(2,128)S(1)} %apply.3), channel_id=1, replica_groups=mesh['freq'=4,'rows'=8] {'rows'}, dimensions={0} | all-to-all | bytes 131072 | tf_op jit(solution)/shard_map/all_to_all | solution.py:264
  72.7 7.2 %apply.4 = f32[8,2,1024]{2,1,0:T(2,128)S(1)} custom-call(s32[1]{0:T(128)S(6)} %copy.6.q_ref, f32[8,2,1024]{2,1,0:T(2,128)S(1)} %all_to_all.26.z_ref, bf16[2,8,8192,128]{3,2,1,0:T(8,128)(2,1)S(1)} %get-tuple-element.10.hi_ref, f8e4m3fn[2,8192,1024]{2,1,0:T(32,128)(4,1)S(1)} %get-tuple-element.11.lo_ref), custom_call_target="tpu_custom_call" | custom-call | tf_op jit(solution)/shard_map/apply/pallas_call | solution.py:235
  79.9 8.3 %all_to_all.27.z_ref = f32[8,2,1024]{2,1,0:T(2,128)S(1)} all-to-all(f32[8,2,1024]{2,1,0:T(2,128)S(1)} %apply.4), channel_id=1, replica_groups=mesh['freq'=4,'rows'=8] {'rows'}, dimensions={0} | all-to-all | bytes 131072 | tf_op jit(solution)/shard_map/all_to_all | solution.py:264
  88.2 7.3 %apply.5 = (f32[2,1024]{1,0:T(2,128)S(1)}, f32[8,8,128]{2,1,0:T(8,128)S(1)}) custom-call(s32[1]{0:T(128)S(6)} %copy.6.q_ref, f32[8,2,1024]{2,1,0:T(2,128)S(1)} %all_to_all.27.z_ref, bf16[2,8,8192,128]{3,2,1,0:T(8,128)(2,1)S(1)} %get-tuple-element.10.hi_ref, f8e4m3fn[2,8192,1024]{2,1,0:T(32,128)(4,1)S(1)} %get-tuple-element.11.lo_ref), custom_call_target="tpu_custom_call" | custom-call | tf_op jit(solution)/shard_map/apply/pallas_call | solution.py:235
  95.5 0.0 copy-start
  95.5 8.1 %all_to_all.28.sums_ref = f32[8,8,128]{2,1,0:T(8,128)S(1)} all-to-all(f32[8,8,128]{2,1,0:T(8,128)S(1)} %get-tuple-element.13), channel_id=1, replica_groups=mesh['freq'=4,'rows'=8] {'rows'}, dimensions={0} | all-to-all | bytes 65536 | tf_op jit(solution)/shard_map/all_to_all | solution.py:264
  103.6 0.0 copy-done
  103.6 1.4 %finish.1 = (f32[2,1024]{1,0:T(2,128)}, f32[1,128]{1,0:T(1,128)}) custom-call(f32[2,1024]{1,0:T(2,128)} %copy-done, f32[8,8,128]{2,1,0:T(8,128)S(1)} %all_to_all.28.sums_ref), custom_call_target="tpu_custom_call" | custom-call | tf_op jit(solution)/shard_map/finish/pallas_call | solution.py:254
Async XLA Ops:
  2.0 12.3 %all-to-all-start = ((f32[8,2,1024]{2,1,0:T(2,128)}), f32[8,2,1024]{2,1,0:T(2,128)S(1)}, u32[]{:S(2)}, u32[]{:S(2)}) async-start(f32[8,2,1024]{2,1,0:T(2,128)} %broadcast_in_dim.8), calls=%async_computation | async-start | bytes 131072 | tf_op jit(solution)/shard_map/all_to_all | solution.py:264
  95.5 8.1 %copy-start = (f32[2,1024]{1,0:T(2,128)}, f32[2,1024]{1,0:T(2,128)S(1)}, u32[]{:S(2)}) copy-start(f32[2,1024]{1,0:T(2,128)S(1)} %get-tuple-element.12.y_ref) | copy-start | bytes 24580

commit v5 on v4

--- a/solution.py
+++ b/solution.py
@@ -21,7 +21,7 @@
 ANY = pl.BlockSpec(memory_space=pl.ANY)
 SUB, LANE, FINE = 8, 128, 8
 GRANT = 17 * 2**19
-CHUNK = 4096
+CHUNK = 8192
 SLAB = 512
 
 

time: 105 us -> 104 us (level)
  Pallas kernels: 57.7 us -> 56.3 us
    pallas_call x3, Pallas kernels: 21.6 us -> 20.2 us  [apply(): pl.pallas_call(functools.partial(kernel, min(CHUNK, nodes)), out_shape=tu...]
where the time goes in v5:
time: 104 us
  Pallas kernels  56.3 us (54%)
  blocking collectives  33 us (32%)
  starting transfers between devices  6.35 us (6%)
  waiting for transfers between devices  5.27 us (5%)
  local copies, waits for them, and re-layouts  1.33 us (1%)
  between operations  1.32 us (1%)
    pallas_call x1, Pallas kernels, first(): pl.pallas_call(functools.partial(first_kernel, slab), out_shape=(pltpu.VM...  34.7 us
    all_to_all x4, blocking collectives, copies_of_all(): return lax.all_to_all(value, 'rows', 0, 0, tiled=True)  33 us
    pallas_call x3, Pallas kernels, apply(): pl.pallas_call(functools.partial(kernel, min(CHUNK, nodes)), out_shape=tu...  20.2 us
    all_to_all x1, starting transfers between devices, copies_of_all(): return lax.all_to_all(value, 'rows', 0, 0, tiled=True)  6.35 us
    all_to_all x1, waiting for transfers between devices, copies_of_all(): return lax.all_to_all(value, 'rows', 0, 0, tiled=True)  5.27 us
  transfers between devices with their start and end apart: 1, of which 1 were waited for; matrix products, arithmetic and copies ran while one was open for 0% of the time, Pallas kernels for 0%

profile of v5, /device:TPU:0, one launch (start us, length us, event | category | flops | bytes accessed | tf_op | source)
XLA Modules:
  0.0 103.6 jit_solution(15597756052066443666)
XLA Ops:
  0.6 1.3 %broadcast_in_dim.8 = f32[8,2,1024]{2,1,0:T(2,128)} broadcast(f32[2,1024]{1,0:T(2,128)} %bitcast.3), dimensions={1,2} | broadcast | bytes 73728 | tf_op jit(solution)/shard_map/broadcast_in_dim | solution.py:280
  2.0 6.4 %all-to-all-start = ((f32[8,2,1024]{2,1,0:T(2,128)}), f32[8,2,1024]{2,1,0:T(2,128)S(1)}, u32[]{:S(2)}, u32[]{:S(2)}) async-start(f32[8,2,1024]{2,1,0:T(2,128)} %broadcast_in_dim.8), calls=%async_computation | async-start | bytes 131072 | tf_op jit(solution)/shard_map/all_to_all | solution.py:264
  9.0 5.3 %all-to-all-done.z_ref = f32[8,2,1024]{2,1,0:T(2,128)S(1)} async-done(((f32[8,2,1024]{2,1,0:T(2,128)}), f32[8,2,1024]{2,1,0:T(2,128)S(1)}, u32[]{:S(2)}, u32[]{:S(2)}) %all-to-all-start) | async-done | bytes 65568 | tf_op jit(solution)/shard_map/all_to_all | solution.py:264
  14.2 34.7 %first.1 = (bf16[2,8,8192,128]{3,2,1,0:T(8,128)(2,1)S(1)}, f8e4m3fn[2,8192,1024]{2,1,0:T(32,128)(4,1)S(1)}, f32[8,2,1024]{2,1,0:T(2,128)S(1)}) custom-call(s32[1]{0:T(128)S(6)} %copy.6.q_ref, f32[8,2,1024]{2,1,0:T(2,128)S(1)} %all-to-all-done.z_ref, bf16[1024,8192]{1,0:T(8,128)(2,1)} %c_hbm.1, s32[1024,8192]{1,0:T(8,128)} %d_hbm.1), custom_call_target="tpu_custom_call" | custom-call | tf_op jit(solution)/shard_map/first/pallas_call | solution.py:209
  49.0 8.3 %all_to_all.25.z_ref = f32[8,2,1024]{2,1,0:T(2,128)S(1)} all-to-all(f32[8,2,1024]{2,1,0:T(2,128)S(1)} %get-tuple-element.9), channel_id=1, replica_groups=mesh['freq'=4,'rows'=8] {'rows'}, dimensions={0} | all-to-all | bytes 131072 | tf_op jit(solution)/shard_map/all_to_all | solution.py:264
  57.3 6.7 %apply.3 = f32[8,2,1024]{2,1,0:T(2,128)S(1)} custom-call(s32[1]{0:T(128)S(6)} %copy.6.q_ref, f32[8,2,1024]{2,1,0:T(2,128)S(1)} %all_to_all.25.z_ref, bf16[2,8,8192,128]{3,2,1,0:T(8,128)(2,1)S(1)} %get-tuple-element.10.hi_ref, f8e4m3fn[2,8192,1024]{2,1,0:T(32,128)(4,1)S(1)} %get-tuple-element.11.lo_ref), custom_call_target="tpu_custom_call" | custom-call | tf_op jit(solution)/shard_map/apply/pallas_call | solution.py:235
  64.0 8.3 %all_to_all.26.z_ref = f32[8,2,1024]{2,1,0:T(2,128)S(1)} all-to-all(f32[8,2,1024]{2,1,0:T(2,128)S(1)} %apply.3), channel_id=1, replica_groups=mesh['freq'=4,'rows'=8] {'rows'}, dimensions={0} | all-to-all | bytes 131072 | tf_op jit(solution)/shard_map/all_to_all | solution.py:264
  72.3 6.7 %apply.4 = f32[8,2,1024]{2,1,0:T(2,128)S(1)} custom-call(s32[1]{0:T(128)S(6)} %copy.6.q_ref, f32[8,2,1024]{2,1,0:T(2,128)S(1)} %all_to_all.26.z_ref, bf16[2,8,8192,128]{3,2,1,0:T(8,128)(2,1)S(1)} %get-tuple-element.10.hi_ref, f8e4m3fn[2,8192,1024]{2,1,0:T(32,128)(4,1)S(1)} %get-tuple-element.11.lo_ref), custom_call_target="tpu_custom_call" | custom-call | tf_op jit(solution)/shard_map/apply/pallas_call | solution.py:235
  79.0 8.3 %all_to_all.27.z_ref = f32[8,2,1024]{2,1,0:T(2,128)S(1)} all-to-all(f32[8,2,1024]{2,1,0:T(2,128)S(1)} %apply.4), channel_id=1, replica_groups=mesh['freq'=4,'rows'=8] {'rows'}, dimensions={0} | all-to-all | bytes 131072 | tf_op jit(solution)/shard_map/all_to_all | solution.py:264
  87.3 6.8 %apply.5 = (f32[2,1024]{1,0:T(2,128)S(1)}, f32[8,8,128]{2,1,0:T(8,128)S(1)}) custom-call(s32[1]{0:T(128)S(6)} %copy.6.q_ref, f32[8,2,1024]{2,1,0:T(2,128)S(1)} %all_to_all.27.z_ref, bf16[2,8,8192,128]{3,2,1,0:T(8,128)(2,1)S(1)} %get-tuple-element.10.hi_ref, f8e4m3fn[2,8192,1024]{2,1,0:T(32,128)(4,1)S(1)} %get-tuple-element.11.lo_ref), custom_call_target="tpu_custom_call" | custom-call | tf_op jit(solution)/shard_map/apply/pallas_call | solution.py:235
  94.1 0.0 copy-start
  94.1 8.1 %all_to_all.28.sums_ref = f32[8,8,128]{2,1,0:T(8,128)S(1)} all-to-all(f32[8,8,128]{2,1,0:T(8,128)S(1)} %get-tuple-element.13), channel_id=1, replica_groups=mesh['freq'=4,'rows'=8] {'rows'}, dimensions={0} | all-to-all | bytes 65536 | tf_op jit(solution)/shard_map/all_to_all | solution.py:264
  102.2 0.0 copy-done
  102.2 1.4 %finish.1 = (f32[2,1024]{1,0:T(2,128)}, f32[1,128]{1,0:T(1,128)}) custom-call(f32[2,1024]{1,0:T(2,128)} %copy-done, f32[8,8,128]{2,1,0:T(8,128)S(1)} %all_to_all.28.sums_ref), custom_call_target="tpu_custom_call" | custom-call | tf_op jit(solution)/shard_map/finish/pallas_call | solution.py:254
Async XLA Ops:
  2.0 12.3 %all-to-all-start = ((f32[8,2,1024]{2,1,0:T(2,128)}), f32[8,2,1024]{2,1,0:T(2,128)S(1)}, u32[]{:S(2)}, u32[]{:S(2)}) async-start(f32[8,2,1024]{2,1,0:T(2,128)} %broadcast_in_dim.8), calls=%async_computation | async-start | bytes 131072 | tf_op jit(solution)/shard_map/all_to_all | solution.py:264
  94.1 8.1 %copy-start = (f32[2,1024]{1,0:T(2,128)}, f32[2,1024]{1,0:T(2,128)S(1)}, u32[]{:S(2)}) copy-start(f32[2,1024]{1,0:T(2,128)S(1)} %get-tuple-element.12.y_ref) | copy-start | bytes 24580
